TPU v7x, 32 devices: a whole 2x2x4 slice. The times are simulated.
32 devices in a mesh: fluid: 4 (over y, x), solid: 8 (over z, core).
Axes of the slice: x: 2, y: 2, z: 4, core: 2. Of those that a mesh axis runs over, the one named last changes fastest.
Arguments:
- fluid_flux: bfloat16 [3, 2048, 128], P(None, ('fluid', 'solid')), may hold values from -6 to 6
- margin_blocks: bfloat16 [5120, 128, 128], P(('fluid', 'solid')), may hold values from 0 to 0.046875
- block_fluid: int32 [5120], P(('fluid', 'solid')), may hold values from 0 to 63
- block_solid: int32 [5120], P(('fluid', 'solid')), may hold values from 0 to 255, as said below
- diag_blocks: float32 [256, 128, 128], P('solid'), may hold values from -3 to 18, as said below
- couple_blocks: float32 [256, 128, 128], P('solid'), may hold values from -0.15 to 0.15
- couple_offset: int32 [256], P('solid'), may hold values from 1 to 16
Outputs:
- mapped: float32 [3, 256, 128], P(None, 'solid')
- nodal: float32 [3, 256, 128], P(None, 'solid')
Inputs may be any that keep to these rules, and one draw needn't show every extreme that they name: `block_solid`: the solid tiles of solid index s are s * 32 to (s + 1) * 32 - 1. Among the 160 blocks of one device at most 50 have solid tiles of one solid index, and exactly 50 do for some index. block_fluid indexes the 64 fluid tiles of the device that holds the block. `diag_blocks`: each diagonal block is symmetric.
All inputs are finite; a program needn't handle non-finite values.
Results may differ from a plain program's by a relative error of at most 0.0003.
Values sent between devices are 32-bit elements; how exact they have to be, the bound alone decides.
A program may use at most 64 MiB of HBM per device.

v0:
```python
import jax
import jax.numpy as jnp
from jax import lax
from jax.sharding import PartitionSpec as P

ITERS = 3


highest = lax.Precision.HIGHEST


def from_behind(block, axis, distance):
    devices = range(lax.axis_size(axis))
    route = [(i - distance, i) for i in devices if i - distance in devices]
    return lax.ppermute(block, axis, route)


def apply_mass(vector, diag_blocks, couple_blocks, couple_offset):
    fields = vector.shape[0]
    own_tiles = vector.shape[1]
    reach = own_tiles // 2
    own_part = jnp.einsum("tij,ftj->fti", diag_blocks, vector, precision=highest)
    ahead_rim = from_behind(vector[:, :reach], "solid", -1)
    padded = jnp.concatenate([vector, ahead_rim], axis=1)
    picked = jnp.zeros_like(vector)
    for offset in range(1, reach + 1):
        offset_hit = (couple_offset == offset)[None, :, None]
        picked = picked + jnp.where(offset_hit, padded[:, offset : offset + own_tiles], 0.0)
    ahead_part = jnp.einsum("tij,ftj->fti", couple_blocks, picked, precision=highest)
    back_terms = jnp.einsum("tji,ftj->fti", couple_blocks, vector, precision=highest)
    spread = jnp.zeros((fields, own_tiles + reach, vector.shape[2]), jnp.float32)
    for offset in range(1, reach + 1):
        offset_hit = (couple_offset == offset)[None, :, None]
        moved = jnp.where(offset_hit, back_terms, 0.0)
        spread = spread + jnp.pad(moved, ((0, 0), (offset, reach - offset), (0, 0)))
    incoming = from_behind(spread[:, own_tiles:], "solid", 1)
    incoming = jnp.pad(incoming, ((0, 0), (0, own_tiles - reach), (0, 0)))
    return own_part + ahead_part + spread[:, :own_tiles] + incoming


def field_dots(first, second):
    return jnp.sum(first * second, axis=(1, 2))


def two_products(residual, image_field):
    return lax.psum((field_dots(residual, residual), field_dots(residual, image_field)), "solid")


def local(
    fluid_flux, margin_blocks, block_fluid, block_solid, diag_blocks, couple_blocks, couple_offset
):
    fields = fluid_flux.shape[0]
    tile_width = fluid_flux.shape[2]
    owners = lax.axis_size("solid")
    own_tiles = diag_blocks.shape[0]
    block_count = block_fluid.shape[0]
    chosen = jnp.take(fluid_flux, block_fluid, axis=1)
    block_terms = jnp.einsum(
        "fbi,bij->bfj", chosen, margin_blocks, preferred_element_type=jnp.float32
    )
    capacity = 5 * block_count // (2 * owners)
    target = block_solid // own_tiles
    local_tile = block_solid - target * own_tiles
    owner_hits = (target[:, None] == jnp.arange(owners, dtype=jnp.int32)[None, :]).astype(jnp.int32)
    slot_rank = jnp.sum((jnp.cumsum(owner_hits, axis=0) - owner_hits) * owner_hits, axis=1)
    slot_index = target * capacity + slot_rank
    values = (
        jnp.zeros((owners * capacity, fields, tile_width), jnp.float32)
        .at[slot_index]
        .set(block_terms)
    )
    labels = jnp.full((owners * capacity,), -1, jnp.int32).at[slot_index].set(local_tile)
    values = values.reshape(owners, capacity, fields, tile_width)
    labels = labels.reshape(owners, capacity)
    values, labels = (
        lax.all_to_all(values, "solid", split_axis=0, concat_axis=0, tiled=True),
        lax.all_to_all(labels, "solid", split_axis=0, concat_axis=0, tiled=True),
    )
    onehot = (
        labels.reshape(-1)[None, :] == jnp.arange(own_tiles, dtype=jnp.int32)[:, None]
    ).astype(jnp.float32)
    partial_value = jnp.einsum(
        "tk,kfj->tfj", onehot, values.reshape(-1, fields, tile_width), precision=highest
    )
    mapped = lax.psum(partial_value, "fluid").transpose(1, 0, 2)
    solution = jnp.zeros_like(mapped)
    residual = mapped
    image_field = apply_mass(residual, diag_blocks, couple_blocks, couple_offset)
    norm_now, product = two_products(residual, image_field)
    step_size = norm_now / product
    direction = residual
    along = image_field
    for iteration in range(ITERS):
        solution = solution + step_size[:, None, None] * direction
        residual = residual - step_size[:, None, None] * along
        if iteration + 1 < ITERS:
            image_field = apply_mass(residual, diag_blocks, couple_blocks, couple_offset)
            norm_next, product = two_products(residual, image_field)
            beta_ratio = norm_next / norm_now
            step_size = norm_next / (product - beta_ratio * norm_next / step_size)
            direction = residual + beta_ratio[:, None, None] * direction
            along = image_field + beta_ratio[:, None, None] * along
            norm_now = norm_next
    return (mapped, solution)


def solution(mesh):
    in_specs = (
        P(None, ("fluid", "solid"), None),
        P(("fluid", "solid"), None, None),
        P(("fluid", "solid")),
        P(("fluid", "solid")),
        P("solid", None, None),
        P("solid", None, None),
        P("solid"),
    )
    out_specs = (P(None, "solid", None), P(None, "solid", None))
    return jax.shard_map(local, mesh=mesh, in_specs=in_specs, out_specs=out_specs, check_vma=False)
```

profile of v0, /device:TPU:0, one launch (start us, length us, event | category | flops | bytes accessed | tf_op | source)
XLA Modules:
  0.0 150.7 jit_solution(7624168068051802495)
XLA Ops:
  0.6 0.8 multiply_subtract_fusion.2
  2.5 1.1 scatter_custom_fusion
  3.6 0.7 all_to_all.9
  4.2 6.4 %all-to-all-start = ((s32[8,1,50]{2,1,0:T(1,128)}), s32[8,1,50]{2,1,0:T(1,128)S(1)}, u32[]{:S(2)}, u32[]{:S(2)}) async-start(s32[8,1,50]{2,1,0:T(1,128)} %all_to_all.9), calls=%async_computation | async-start | bytes 8192 | tf_op jit(solution)/shard_map/all_to_all | solution.py:77
  10.6 0.7 compare_select_fusion
  11.3 0.7 compare_and_fusion
  12.0 2.2 %gather_fusion = bf16[160,3,128]{2,0,1:T(8,128)(2,1)S(1)} fusion(bf16[3,64,128]{2,1,0:T(8,128)(2,1)} %param.7, s32[1024]{0:T(1024)S(1)} %pad_clamp_fusion), kind=kCustom, calls=%fused_computation | custom fusion | bytes 246400 | tf_op jit(solution)/shard_map/jit(_take)/gather | solution.py:57
  14.2 3.9 %fusion = f32[160,3,128]{2,1,0:T(4,128)S(1)} fusion(bf16[160,128,128]{2,1,0:T(8,128)(2,1)} %param.8, bf16[3,160,128]{2,1,0:T(8,128)(2,1)S(1)} %select_bitcast_fusion), kind=kOutput, calls=%fused_computation.64 | convolution fusion | flops 15728640 | bytes 5611520 | tf_op jit(solution)/shard_map/fbi,bij->bfj/dot_general | solution.py:58
  18.3 5.3 %scatter_fusion = f32[400,3,128]{2,1,0:T(4,128)S(1)} fusion(f32[400,3,128]{2,1,0:T(4,128)S(1)} %broadcast_in_dim.587, s32[160]{0:T(256)S(1)} %compare_select_fusion.1, f32[160,3,128]{2,1,0:T(4,128)S(1)} %fusion), kind=kCustom, calls=%fused_computation.2 | custom fusion | bytes 737920 | tf_op jit(solution)/shard_map/scatter | solution.py:70
  23.6 0.9 copy.140
  24.5 5.1 %all-to-all-start.1 = ((f32[8,50,3,128]{3,1,2,0:T(8,128)}), f32[8,50,3,128]{3,1,2,0:T(8,128)S(1)}, u32[]{:S(2)}, u32[]{:S(2)}) async-start(f32[8,50,3,128]{3,1,2,0:T(8,128)} %copy.140), calls=%async_computation.1 | async-start | bytes 1376256 | tf_op jit(solution)/shard_map/all_to_all | solution.py:76
  31.5 17.0 %all-to-all-done.1 = f32[8,50,3,128]{3,1,2,0:T(8,128)S(1)} async-done(((f32[8,50,3,128]{3,1,2,0:T(8,128)}), f32[8,50,3,128]{3,1,2,0:T(8,128)S(1)}, u32[]{:S(2)}, u32[]{:S(2)}) %all-to-all-start.1) | async-done | bytes 614432 | tf_op jit(solution)/shard_map/all_to_all | solution.py:76
  49.0 16.8 %psum.49 = f32[3,32,128]{2,1,0:T(8,128)S(1)} all-reduce(f32[3,32,128]{2,1,0:T(8,128)S(1)} %convolution_bitcast_fusion), channel_id=1, replica_groups=mesh['fluid'=4,'solid'=8] {'fluid'}, use_global_device_ids=true, to_apply=%region_5.6 | all-reduce | flops 12288 | bytes 98304 | tf_op jit(solution)/shard_map/psum | solution.py:85
  65.9 1.9 %fusion.10 = f32[32,3,128]{2,1,0:T(4,128)S(1)} fusion(f32[32,128,128]{2,1,0:T(8,128)S(1)} %copy-done, f32[3,32,128]{2,1,0:T(8,128)S(1)} %psum.49), kind=kOutput, calls=%fused_computation.78 | convolution fusion | flops 18874368 | bytes 2195456 | tf_op jit(solution)/shard_map/tji,ftj->fti/dot_general | solution.py:30
  68.2 1.3 collective-permute-start.1
  69.5 1.3 collective-permute-start
  70.8 3.4 %fusion.12 = f32[32,3,128]{2,1,0:T(4,128)S(1)} fusion(f32[32,128,128]{2,1,0:T(8,128)S(1)} %copy-done.1, f32[3,32,128]{2,1,0:T(8,128)S(1)} %psum.49), kind=kOutput, calls=%fused_computation.80 | convolution fusion | flops 18874368 | bytes 2195456 | tf_op jit(solution)/shard_map/tij,ftj->fti/dot_general | solution.py:22
  74.3 3.4 %fusion.18 = f32[32,3,128]{2,1,0:T(4,128)S(1)} fusion(f32[32,128,128]{2,1,0:T(8,128)S(1)} %copy-done, f32[3,32,128]{2,1,0:T(8,128)S(1)} %fusion.119), kind=kOutput, calls=%fused_computation.86 | convolution fusion | flops 18874368 | bytes 2195456 | tf_op jit(solution)/shard_map/tij,ftj->fti/dot_general | solution.py:29
  77.8 16.3 %all-reduce.54 = (f32[3]{0:T(128)S(1)}, f32[3]{0:T(128)S(1)}) all-reduce(f32[3]{0:T(128)S(1)} %get-tuple-element.7, f32[3]{0:T(128)S(1)} %get-tuple-element.6), channel_id=1, replica_groups=mesh['fluid'=4,'solid'=8] {'solid'}, use_global_device_ids=true, to_apply=%region_7.8 | all-reduce | flops 6 | bytes 48 | tf_op jit(solution)/shard_map/psum | solution.py:46
  94.2 1.9 %fusion.6 = f32[32,3,128]{2,1,0:T(4,128)S(1)} fusion(f32[32,128,128]{2,1,0:T(8,128)S(1)} %copy-done, f32[3,32,128]{2,1,0:T(8,128)S(1)} %multiply_subtract_fusion.1), kind=kOutput, calls=%fused_computation.74 | convolution fusion | flops 18874368 | bytes 2195456 | tf_op jit(solution)/shard_map/tji,ftj->fti/dot_general | solution.py:30
  96.1 3.4 %fusion.8 = f32[32,3,128]{2,1,0:T(4,128)S(1)} fusion(f32[32,128,128]{2,1,0:T(8,128)S(1)} %copy-done.2, f32[3,32,128]{2,1,0:T(8,128)S(1)} %multiply_subtract_fusion.1), kind=kOutput, calls=%fused_computation.76 | convolution fusion | flops 18874368 | bytes 2195456 | tf_op jit(solution)/shard_map/tij,ftj->fti/dot_general | solution.py:22
  99.7 1.3 collective-permute-start.2
  101.1 3.0 %collective-permute-start.3 = (f32[3,16,128]{2,1,0:T(8,128)S(1)}, f32[3,16,128]{2,1,0:T(8,128)S(1)}, u32[]{:S(2)}, u32[]{:S(2)}) collective-permute-start(f32[3,16,128]{2,1,0:T(8,128)S(1)} %slice.295), channel_id=1, source_target_pairs={{0,1},{1,2},{2,3},{3,4},{4,5},{5,6},{6,7},{8,9},{9,10},{10,11},{11... | collective-permute-start | bytes 73736 | tf_op jit(solution)/shard_map/ppermute | solution.py:15
  104.3 3.4 %fusion.16 = f32[32,3,128]{2,1,0:T(4,128)S(1)} fusion(f32[32,128,128]{2,1,0:T(8,128)S(1)} %copy-done, f32[3,32,128]{2,1,0:T(8,128)S(1)} %fusion.70), kind=kOutput, calls=%fused_computation.84 | convolution fusion | flops 18874368 | bytes 2195456 | tf_op jit(solution)/shard_map/tij,ftj->fti/dot_general | solution.py:29
  107.8 13.6 %all-reduce.53 = (f32[3]{0:T(128)S(1)}, f32[3]{0:T(128)S(1)}) all-reduce(f32[3]{0:T(128)S(1)} %get-tuple-element.5, f32[3]{0:T(128)S(1)} %get-tuple-element.4), channel_id=1, replica_groups=mesh['fluid'=4,'solid'=8] {'solid'}, use_global_device_ids=true, to_apply=%region_11.12 | all-reduce | flops 6 | bytes 48 | tf_op jit(solution)/shard_map/psum | solution.py:46
  121.5 1.9 %fusion.2 = f32[32,3,128]{2,1,0:T(4,128)S(1)} fusion(f32[32,128,128]{2,1,0:T(8,128)S(1)} %copy-done, f32[3,32,128]{2,1,0:T(8,128)S(1)} %multiply_subtract_fusion), kind=kOutput, calls=%fused_computation.70 | convolution fusion | flops 18874368 | bytes 2195456 | tf_op jit(solution)/shard_map/tji,ftj->fti/dot_general | solution.py:30
  123.4 3.4 %fusion.4 = f32[32,3,128]{2,1,0:T(4,128)S(1)} fusion(f32[32,128,128]{2,1,0:T(8,128)S(1)} %copy-done.3, f32[3,32,128]{2,1,0:T(8,128)S(1)} %multiply_subtract_fusion), kind=kOutput, calls=%fused_computation.72 | convolution fusion | flops 18874368 | bytes 2195456 | tf_op jit(solution)/shard_map/tij,ftj->fti/dot_general | solution.py:22
  127.0 1.3 collective-permute-start.4
  128.4 3.3 %collective-permute-start.5 = (f32[3,16,128]{2,1,0:T(8,128)S(1)}, f32[3,16,128]{2,1,0:T(8,128)S(1)}, u32[]{:S(2)}, u32[]{:S(2)}) collective-permute-start(f32[3,16,128]{2,1,0:T(8,128)S(1)} %slice.328), channel_id=1, source_target_pairs={{0,1},{1,2},{2,3},{3,4},{4,5},{5,6},{6,7},{8,9},{9,10},{10,11},{11... | collective-permute-start | bytes 73736 | tf_op jit(solution)/shard_map/ppermute | solution.py:15
  131.8 3.4 %fusion.14 = f32[32,3,128]{2,1,0:T(4,128)S(1)} fusion(f32[32,128,128]{2,1,0:T(8,128)S(1)} %copy-done, f32[3,32,128]{2,1,0:T(8,128)S(1)} %fusion.25), kind=kOutput, calls=%fused_computation.82 | convolution fusion | flops 18874368 | bytes 2195456 | tf_op jit(solution)/shard_map/tij,ftj->fti/dot_general | solution.py:29
  135.3 14.7 %all-reduce.52 = (f32[3]{0:T(128)S(1)}, f32[3]{0:T(128)S(1)}) all-reduce(f32[3]{0:T(128)S(1)} %get-tuple-element.3, f32[3]{0:T(128)S(1)} %get-tuple-element.2), channel_id=1, replica_groups=mesh['fluid'=4,'solid'=8] {'solid'}, use_global_device_ids=true, to_apply=%region_15.16 | all-reduce | flops 6 | bytes 48 | tf_op jit(solution)/shard_map/psum | solution.py:46
  150.0 0.7 multiply_add_fusion
  (82 shorter events, 5.7 us)
Async XLA Ops:
  0.6 65.2 %copy-start = (f32[32,128,128]{2,1,0:T(8,128)S(1)}, f32[32,128,128]{2,1,0:T(8,128)}, u32[]{:S(2)}) copy-start(f32[32,128,128]{2,1,0:T(8,128)} %param.12) | copy-start | bytes 6291460
  4.2 20.3 %all-to-all-start = ((s32[8,1,50]{2,1,0:T(1,128)}), s32[8,1,50]{2,1,0:T(1,128)S(1)}, u32[]{:S(2)}, u32[]{:S(2)}) async-start(s32[8,1,50]{2,1,0:T(1,128)} %all_to_all.9), calls=%async_computation | async-start | bytes 8192 | tf_op jit(solution)/shard_map/all_to_all | solution.py:77
  18.3 11.3 %copy-start.13 = (s32[32]{0:T(128)S(1)}, s32[32]{0:T(128)}, u32[]{:S(2)}) copy-start(s32[32]{0:T(128)} %param.13) | copy-start | bytes 388
  24.5 23.9 %all-to-all-start.1 = ((f32[8,50,3,128]{3,1,2,0:T(8,128)}), f32[8,50,3,128]{3,1,2,0:T(8,128)S(1)}, u32[]{:S(2)}, u32[]{:S(2)}) async-start(f32[8,50,3,128]{3,1,2,0:T(8,128)} %copy.140), calls=%async_computation.1 | async-start | bytes 1376256 | tf_op jit(solution)/shard_map/all_to_all | solution.py:76
  48.5 19.3 %copy-start.5 = (pred[32]{0:T(512)(128)(4,1)S(1)}, pred[32]{0:T(512)(128)(4,1)}, u32[]{:S(2)}) copy-start(pred[32]{0:T(512)(128)(4,1)} %get-tuple-element.81) | copy-start | bytes 100
  48.5 19.3 %copy-start.6 = (pred[32]{0:T(512)(128)(4,1)S(1)}, pred[32]{0:T(512)(128)(4,1)}, u32[]{:S(2)}) copy-start(pred[32]{0:T(512)(128)(4,1)} %get-tuple-element.82) | copy-start | bytes 100
  48.5 19.3 %copy-start.7 = (pred[32]{0:T(512)(128)(4,1)S(1)}, pred[32]{0:T(512)(128)(4,1)}, u32[]{:S(2)}) copy-start(pred[32]{0:T(512)(128)(4,1)} %get-tuple-element.83) | copy-start | bytes 100
  48.5 19.3 %copy-start.8 = (pred[32]{0:T(512)(128)(4,1)S(1)}, pred[32]{0:T(512)(128)(4,1)}, u32[]{:S(2)}) copy-start(pred[32]{0:T(512)(128)(4,1)} %get-tuple-element.84) | copy-start | bytes 100
  48.5 19.3 %copy-start.9 = (pred[32]{0:T(512)(128)(4,1)S(1)}, pred[32]{0:T(512)(128)(4,1)}, u32[]{:S(2)}) copy-start(pred[32]{0:T(512)(128)(4,1)} %get-tuple-element.85) | copy-start | bytes 100
  48.6 19.3 %copy-start.10 = (pred[32]{0:T(512)(128)(4,1)S(1)}, pred[32]{0:T(512)(128)(4,1)}, u32[]{:S(2)}) copy-start(pred[32]{0:T(512)(128)(4,1)} %get-tuple-element.86) | copy-start | bytes 100
  48.6 19.2 %copy-start.11 = (pred[32]{0:T(512)(128)(4,1)S(1)}, pred[32]{0:T(512)(128)(4,1)}, u32[]{:S(2)}) copy-start(pred[32]{0:T(512)(128)(4,1)} %get-tuple-element.88) | copy-start | bytes 100
  48.6 19.2 %copy-start.12 = (pred[32]{0:T(512)(128)(4,1)S(1)}, pred[32]{0:T(512)(128)(4,1)}, u32[]{:S(2)}) copy-start(pred[32]{0:T(512)(128)(4,1)} %get-tuple-element.89) | copy-start | bytes 100
  65.8 84.2 %copy-start.4 = (f32[3,32,128]{2,1,0:T(8,128)}, f32[3,32,128]{2,1,0:T(8,128)S(1)}, u32[]{:S(2)}) copy-start(f32[3,32,128]{2,1,0:T(8,128)S(1)} %psum.49) | copy-start | bytes 147460
  65.8 4.9 %copy-start.1 = (f32[32,128,128]{2,1,0:T(8,128)S(1)}, f32[32,128,128]{2,1,0:T(8,128)}, u32[]{:S(2)}) copy-start(f32[32,128,128]{2,1,0:T(8,128)} %param.11) | copy-start | bytes 6291460
  68.2 9.5 %collective-permute-start.1 = (f32[3,16,128]{2,1,0:T(8,128)S(1)}, f32[3,16,128]{2,1,0:T(8,128)S(1)}, u32[]{:S(2)}, u32[]{:S(2)}) collective-permute-start(f32[3,16,128]{2,1,0:T(8,128)S(1)} %slice.262), channel_id=1, source_target_pairs={{0,1},{1,2},{2,3},{3,4},{4,5},{5,6},{6,7},{8,9},{9,10},{10,11},{11... | collective-permute-start | bytes 73736 | tf_op jit(solution)/shard_map/ppermute | solution.py:15
  69.5 4.7 %collective-permute-start = (f32[3,16,128]{2,1,0:T(8,128)S(1)}, f32[3,16,128]{2,1,0:T(8,128)S(1)}, u32[]{:S(2)}, u32[]{:S(2)}) collective-permute-start(f32[3,16,128]{2,1,0:T(8,128)S(1)} %slice.244), channel_id=1, source_target_pairs={{1,0},{2,1},{3,2},{4,3},{5,4},{6,5},{7,6},{9,8},{10,9},{11,10},{12... | collective-permute-start | bytes 73736 | tf_op jit(solution)/shard_map/ppermute | solution.py:15
  94.1 2.0 %copy-start.2 = (f32[32,128,128]{2,1,0:T(8,128)S(1)}, f32[32,128,128]{2,1,0:T(8,128)}, u32[]{:S(2)}) copy-start(f32[32,128,128]{2,1,0:T(8,128)} %param.11) | copy-start | bytes 6291460
  99.7 4.5 %collective-permute-start.2 = (f32[3,16,128]{2,1,0:T(8,128)S(1)}, f32[3,16,128]{2,1,0:T(8,128)S(1)}, u32[]{:S(2)}, u32[]{:S(2)}) collective-permute-start(f32[3,16,128]{2,1,0:T(8,128)S(1)} %slice.263), channel_id=1, source_target_pairs={{1,0},{2,1},{3,2},{4,3},{5,4},{6,5},{7,6},{9,8},{10,9},{11,10},{12... | collective-permute-start | bytes 73736 | tf_op jit(solution)/shard_map/ppermute | solution.py:15
  101.1 6.6 %collective-permute-start.3 = (f32[3,16,128]{2,1,0:T(8,128)S(1)}, f32[3,16,128]{2,1,0:T(8,128)S(1)}, u32[]{:S(2)}, u32[]{:S(2)}) collective-permute-start(f32[3,16,128]{2,1,0:T(8,128)S(1)} %slice.295), channel_id=1, source_target_pairs={{0,1},{1,2},{2,3},{3,4},{4,5},{5,6},{6,7},{8,9},{9,10},{10,11},{11... | collective-permute-start | bytes 73736 | tf_op jit(solution)/shard_map/ppermute | solution.py:15
  121.4 2.0 %copy-start.3 = (f32[32,128,128]{2,1,0:T(8,128)S(1)}, f32[32,128,128]{2,1,0:T(8,128)}, u32[]{:S(2)}) copy-start(f32[32,128,128]{2,1,0:T(8,128)} %param.11) | copy-start | bytes 6291460
  127.0 4.7 %collective-permute-start.4 = (f32[3,16,128]{2,1,0:T(8,128)S(1)}, f32[3,16,128]{2,1,0:T(8,128)S(1)}, u32[]{:S(2)}, u32[]{:S(2)}) collective-permute-start(f32[3,16,128]{2,1,0:T(8,128)S(1)} %slice.296), channel_id=1, source_target_pairs={{1,0},{2,1},{3,2},{4,3},{5,4},{6,5},{7,6},{9,8},{10,9},{11,10},{12... | collective-permute-start | bytes 73736 | tf_op jit(solution)/shard_map/ppermute | solution.py:15
  128.4 6.8 %collective-permute-start.5 = (f32[3,16,128]{2,1,0:T(8,128)S(1)}, f32[3,16,128]{2,1,0:T(8,128)S(1)}, u32[]{:S(2)}, u32[]{:S(2)}) collective-permute-start(f32[3,16,128]{2,1,0:T(8,128)S(1)} %slice.328), channel_id=1, source_target_pairs={{0,1},{1,2},{2,3},{3,4},{4,5},{5,6},{6,7},{8,9},{9,10},{10,11},{11... | collective-permute-start | bytes 73736 | tf_op jit(solution)/shard_map/ppermute | solution.py:15
where the time goes:
time: 151 us
  blocking collectives  61.4 us (41%)
  matrix products  30 us (20%)
  starting transfers between devices  22.9 us (15%)
  waiting for transfers between devices  17 us (11%)
  local copies, waits for them, and re-layouts  11.2 us (7%)
  other arithmetic  7.1 us (5%)
    psum x3, blocking collectives, two_products(): lax.psum((field_dots(residual, residual), field_dots(residual, image_fiel...  44.6 us
    all_to_all x1, waiting for transfers between devices, local(): lax.all_to_all(values, 'solid', split_axis=0, concat_axis=0, tiled=True)  17 us
    psum x1, blocking collectives, local(): mapped = lax.psum(partial_value, 'fluid').transpose(1, 0, 2)  16.8 us
    ppermute x6, starting transfers between devices, from_behind(): return lax.ppermute(block, axis, route)  11.5 us
    dot_general x3, matrix products, apply_mass(): jnp.einsum('tij,ftj->fti', diag_blocks, vector, precision=highest)  10.1 us
    dot_general x3, matrix products, apply_mass(): jnp.einsum('tij,ftj->fti', couple_blocks, picked, precision=highest)  10.1 us
    all_to_all x1, starting transfers between devices, local(): lax.all_to_all(labels, 'solid', split_axis=0, concat_axis=0, tiled=True)  6.35 us
    dot_general x3, matrix products, apply_mass(): jnp.einsum('tji,ftj->fti', couple_blocks, vector, precision=highest)  5.58 us
  transfers between devices with their start and end apart: 8, of which 1 were waited for; matrix products, arithmetic and copies ran while one was open for 20% of the time, Pallas kernels for 0%

commit v1 on v0

v1 whole, which is shorter than its diff:
```python
import functools

import jax
import jax.numpy as jnp
from jax import lax
from jax.experimental import pallas as pl
from jax.experimental.pallas import tpu as pltpu
from jax.sharding import PartitionSpec as P

MESH = pl.DeviceIdType.MESH
ROWS = 8
LANES = 128


def gather_kernel(fluids, owners, chunks, group, fluid_ids, solid_ids, flux, blocks, out, faces, total):
    step = pl.program_id(0)
    fields = flux.shape[0]
    per_step = blocks.shape[0]
    own_tiles = chunks * fluids

    @pl.when(step == 0)
    def _():
        total[...] = jnp.zeros_like(total)
        faces[...] = jnp.zeros_like(faces)
        for field in range(fields):
            faces[pl.ds(field, flux.shape[1], stride=ROWS), :] = flux[field].astype(jnp.float32)

    def some(index, carry):
        terms = []
        for inner in range(group):
            here = index * group + inner
            start = pl.multiple_of(fluid_ids[step * per_step + here] * ROWS, ROWS)
            chosen = faces[pl.ds(start, ROWS), :].astype(jnp.bfloat16)
            terms.append(jnp.dot(chosen, blocks[here], preferred_element_type=jnp.float32))
        for inner in range(group):
            here = index * group + inner
            start = pl.multiple_of(solid_ids[step * per_step + here] * ROWS, ROWS)
            total[pl.ds(start, ROWS), :] += terms[inner]
        return carry

    lax.fori_loop(0, per_step // group, some, 0)

    @pl.when(step == pl.num_programs(0) - 1)
    def _():
        def one_owner(owner, carry):
            for part in range(fluids):
                for field in range(fields):
                    start = (owner * own_tiles + part * chunks) * ROWS + field
                    out[part, owner, field] = total[pl.ds(start, chunks, stride=ROWS), :]
            return carry

        lax.fori_loop(0, owners, one_owner, 0)


def gather_terms(flux, blocks, fluid_ids, solid_ids, fluids, owners, own_tiles):
    fields, fluid_tiles, width = flux.shape
    count = blocks.shape[0]
    steps = 4 if count % 32 == 0 else 1
    chunks = own_tiles // fluids
    return pl.pallas_call(
        functools.partial(gather_kernel, fluids, owners, chunks, 8),
        grid=(steps,),
        out_shape=jax.ShapeDtypeStruct((fluids, owners, fields, chunks, width), jnp.float32),
        in_specs=[
            pl.BlockSpec(memory_space=pltpu.SMEM),
            pl.BlockSpec(memory_space=pltpu.SMEM),
            pl.BlockSpec(memory_space=pltpu.VMEM),
            pl.BlockSpec((count // steps, width, width), lambda i: (i, 0, 0)),
        ],
        out_specs=pl.BlockSpec(memory_space=pltpu.VMEM),
        scratch_shapes=[
            pltpu.VMEM((fluid_tiles * ROWS, width), jnp.float32),
            pltpu.VMEM((owners * own_tiles * ROWS, width), jnp.float32),
        ],
        name="gather_terms",
    )(fluid_ids, solid_ids, flux, blocks)


def halves(value):
    high = value.astype(jnp.bfloat16)
    low = (value - high.astype(jnp.float32)).astype(jnp.bfloat16)
    return high, low


def stacked(value):
    both = jnp.concatenate(halves(value), axis=0)
    return jnp.concatenate([both, both], axis=1)


def folded(product):
    return product[:ROWS] + product[ROWS:]


def project_kernel(
    fluids, owners, offsets, parts, offset_rows, diag, couple, mapped_out, nodal_out,
    diag_f, couple_f, first, second, got_fluid, to_owner, got_owner, mapped,
    basis0, basis1, basis2, picks, spread, back, rim_out, rim_in, carry_out, carry_in, sums,
    load_sem, send1, recv1, send2, recv2, send3, recv3, send_rim, recv_rim,
    send_carry, recv_carry, send_sum, recv_sum,
):
    me_g = lax.axis_index("fluid")
    me_s = lax.axis_index("solid")
    fields = parts.shape[2]
    chunks = parts.shape[3]
    own_tiles = diag.shape[0]
    reach = own_tiles // 2
    own_rows = own_tiles * ROWS

    load_d = pltpu.make_async_copy(diag, diag_f, load_sem.at[0])
    load_c = pltpu.make_async_copy(couple, couple_f, load_sem.at[1])
    load_d.start()
    load_c.start()

    def fluid_peer(step):
        return lax.rem(me_g + step, fluids)

    def solid_peer(step):
        return lax.rem(me_s + step, owners)

    barrier = pltpu.get_barrier_semaphore()
    for step in range(1, fluids):
        pl.semaphore_signal(
            barrier, inc=1, device_id={"fluid": fluid_peer(step), "solid": me_s}, device_id_type=MESH
        )
    for step in range(1, owners):
        pl.semaphore_signal(
            barrier, inc=1, device_id={"fluid": me_g, "solid": solid_peer(step)}, device_id_type=MESH
        )
    pl.semaphore_wait(barrier, fluids - 1 + owners - 1)

    def remote(src, dst, send_sem, recv_sem, g, s):
        return pltpu.make_async_remote_copy(
            src_ref=src, dst_ref=dst, send_sem=send_sem, recv_sem=recv_sem,
            device_id={"fluid": g, "solid": s}, device_id_type=MESH,
        )

    def copy1(hop, step):
        owner = solid_peer(step)
        peer = fluid_peer(hop)
        return remote(
            parts.at[peer, owner], got_fluid.at[hop - 1, owner],
            send1.at[hop - 1, owner], recv1.at[hop - 1, owner], peer, me_s,
        )

    def copy2(step):
        owner = solid_peer(step)
        return remote(
            to_owner.at[step - 1], got_owner.at[step - 1],
            send2.at[step - 1], recv2.at[step - 1], me_g, owner,
        )

    def copy3(hop):
        return remote(
            mapped.at[me_g], mapped.at[me_g], send3.at[hop - 1], recv3.at[hop - 1], fluid_peer(hop), me_s
        )

    def copy_sum(step):
        return remote(
            sums.at[me_s], sums.at[me_s], send_sum.at[step - 1], recv_sum.at[step - 1],
            me_g, solid_peer(step),
        )

    for step in range(1, owners + 1):
        for hop in range(1, fluids):
            copy1(hop, step).start()

    basis0[...] = jnp.zeros_like(basis0)
    basis1[...] = jnp.zeros_like(basis1)
    basis2[...] = jnp.zeros_like(basis2)

    load_d.wait()
    load_c.wait()

    def prepare(tile, carry):
        diag_high, diag_low = halves(diag_f[tile])
        block = couple_f[tile]
        couple_high, couple_low = halves(block)
        turned_high, turned_low = halves(block.T)
        first[tile, :LANES, :LANES] = diag_high
        first[tile, LANES:, :LANES] = diag_low
        first[tile, :LANES, LANES:] = couple_high
        first[tile, LANES:, LANES:] = couple_low
        second[tile, :LANES, :] = turned_high
        second[tile, LANES:, :] = turned_low
        return carry

    lax.fori_loop(0, own_tiles, prepare, 0)

    for step in range(1, owners + 1):
        owner = solid_peer(step)
        for hop in range(1, fluids):
            copy1(hop, step).wait_recv()
        total = parts[me_g, owner]
        for hop in range(1, fluids):
            total = total + got_fluid[hop - 1, owner]
        if step < owners:
            to_owner[step - 1] = total
            copy2(step).start()
    for step in range(1, owners):
        copy2(step).wait_recv()
        total = total + got_owner[step - 1]
    mapped[me_g] = total
    for hop in range(1, fluids):
        copy3(hop).start()
    for hop in range(1, fluids):
        copy3(hop).wait_recv()
    for part in range(fluids):
        for field in range(fields):
            values = mapped[part, field]
            mapped_out[field, part * chunks : (part + 1) * chunks, :] = values
            basis0[pl.ds(part * chunks * ROWS + field, chunks, stride=ROWS), :] = values

    def rim_copy(turn):
        return remote(
            rim_out.at[turn], rim_in.at[turn], send_rim.at[turn], recv_rim.at[turn], me_g, me_s - 1
        )

    def carry_copy(turn):
        return remote(
            carry_out.at[turn], carry_in.at[turn], send_carry.at[turn], recv_carry.at[turn], me_g, me_s + 1
        )

    def send_rim_of(turn, vector):
        for field in range(fields):
            rim_out[turn, field] = vector[pl.ds(field, reach, stride=ROWS), :]

        @pl.when(me_s > 0)
        def _():
            rim_copy(turn).start()

    def take_rim(turn, vector):
        @pl.when(me_s < owners - 1)
        def _():
            rim_copy(turn).wait_recv()
            for field in range(fields):
                vector[pl.ds(own_rows + field, reach, stride=ROWS), :] = rim_in[turn, field]

        for tile in range(own_tiles + reach):
            picks[tile] = vector[tile * ROWS : (tile + 1) * ROWS, :]

    def rows_of(tile):
        return pl.ds(pl.multiple_of(tile * ROWS, ROWS), ROWS)

    def ahead_of(tile):
        picked = picks[tile + offsets[tile]]
        return folded(jnp.dot(stacked(picked), second[tile], preferred_element_type=jnp.float32))

    def apply_mass(turn, vector, image):
        send_rim_of(turn, vector)

        def own(tile, carry):
            product = folded(
                jnp.dot(stacked(vector[rows_of(tile), :]), first[tile], preferred_element_type=jnp.float32)
            )
            spread[rows_of(tile), :] = product[:, :LANES]
            back[rows_of(tile), :] = product[:, LANES:]
            return carry

        lax.fori_loop(0, own_tiles, own, 0, unroll=8)
        spread[own_rows:, :] = jnp.zeros((reach * ROWS, LANES), jnp.float32)

        def move(offset, carry):
            start = pl.multiple_of(offset * ROWS, ROWS)
            moved = jnp.where(offset_rows[...] == offset, back[...], 0.0)
            spread[pl.ds(start, own_rows), :] += moved
            return carry

        lax.fori_loop(1, reach + 1, move, 0)
        for field in range(fields):
            carry_out[turn, field] = spread[pl.ds(own_rows + field, reach, stride=ROWS), :]

        @pl.when(me_s < owners - 1)
        def _():
            carry_copy(turn).start()

        take_rim(turn, vector)

        def ahead(tile, carry):
            image[rows_of(tile), :] = spread[rows_of(tile), :] + ahead_of(tile)
            return carry

        lax.fori_loop(0, own_tiles, ahead, 0, unroll=8)

        @pl.when(me_s > 0)
        def _():
            carry_copy(turn).wait_recv()
            for field in range(fields):
                image[pl.ds(field, reach, stride=ROWS), :] += carry_in[turn, field]

    apply_mass(0, basis0, basis1)
    apply_mass(1, basis1, basis2)
    send_rim_of(2, basis2)

    def dots(tile, carry):
        zero, one, two = (b[rows_of(tile), :] for b in (basis0, basis1, basis2))
        product = folded(
            jnp.dot(stacked(two), first[tile, :, :LANES], preferred_element_type=jnp.float32)
        )
        pairs = ((zero, zero), (zero, one), (one, one), (one, two), (two, two), (two, product))
        return tuple(c + a * b for c, (a, b) in zip(carry, pairs))

    nothing = jnp.zeros((ROWS, LANES), jnp.float32)
    products = lax.fori_loop(0, own_tiles, dots, (nothing,) * 6, unroll=8)
    take_rim(2, basis2)

    def last(tile, carry):
        return carry + 2.0 * basis2[rows_of(tile), :] * ahead_of(tile)

    products = products[:5] + (lax.fori_loop(0, own_tiles, last, products[5], unroll=8),)
    lane = lax.broadcasted_iota(jnp.int32, (ROWS, LANES), 1)
    packed = nothing
    for place, product in enumerate(products):
        packed = jnp.where(lane == place, jnp.sum(product, axis=1, keepdims=True), packed)
    sums[me_s] = packed
    for step in range(1, owners):
        copy_sum(step).start()
    for step in range(1, owners):
        copy_sum(step).wait_recv()
    everyone = sums[0]
    for device in range(1, owners):
        everyone = everyone + sums[device]
    moments = [
        jnp.sum(jnp.where(lane == place, everyone, 0.0), axis=1, keepdims=True) for place in range(6)
    ]

    def form(coefficients, shift):
        total = None
        for i, left in enumerate(coefficients):
            for j, right in enumerate(coefficients):
                term = left * right * moments[i + j + shift]
                total = term if total is None else total + term
        return total

    alpha0 = moments[0] / moments[1]
    residual1 = (1.0, -alpha0)
    norm1 = form(residual1, 0)
    beta0 = norm1 / moments[0]
    direction1 = (1.0 + beta0, -alpha0)
    alpha1 = norm1 / form(direction1, 1)
    residual2 = (1.0, -alpha0 - alpha1 * direction1[0], -alpha1 * direction1[1])
    norm2 = form(residual2, 0)
    beta1 = norm2 / norm1
    direction2 = (
        residual2[0] + beta1 * direction1[0], residual2[1] + beta1 * direction1[1], residual2[2]
    )
    alpha2 = norm2 / form(direction2, 1)
    weights = (
        alpha0 + alpha1 * direction1[0] + alpha2 * direction2[0],
        alpha1 * direction1[1] + alpha2 * direction2[1],
        alpha2 * direction2[2],
    )
    for field in range(fields):
        result = None
        for weight, vector in zip(weights, (basis0, basis1, basis2)):
            term = weight[field : field + 1] * vector[pl.ds(field, own_tiles, stride=ROWS), :]
            result = term if result is None else result + term
        nodal_out[field] = result

    for step in range(1, owners + 1):
        for hop in range(1, fluids):
            copy1(hop, step).wait_send()
    for step in range(1, owners):
        copy2(step).wait_send()
        copy_sum(step).wait_send()
    for hop in range(1, fluids):
        copy3(hop).wait_send()

    @pl.when(me_s > 0)
    def _():
        for turn in range(3):
            rim_copy(turn).wait_send()

    @pl.when(me_s < owners - 1)
    def _():
        for turn in range(2):
            carry_copy(turn).wait_send()


def project(parts, diag, couple, offsets):
    fluids, owners, fields, chunks, width = parts.shape
    own_tiles = diag.shape[0]
    reach = own_tiles // 2
    offset_rows = jnp.broadcast_to(offsets[:, None, None], (own_tiles, ROWS, width))
    offset_rows = offset_rows.reshape(own_tiles * ROWS, width)
    f32, bf16 = jnp.float32, jnp.bfloat16
    dma = pltpu.SemaphoreType.DMA
    wide = (own_tiles + reach) * ROWS
    out = jax.ShapeDtypeStruct((fields, own_tiles, width), f32)
    vmem = pl.BlockSpec(memory_space=pltpu.VMEM)
    return pl.pallas_call(
        functools.partial(project_kernel, fluids, owners),
        out_shape=(out, out),
        in_specs=[
            pl.BlockSpec(memory_space=pltpu.SMEM), vmem, vmem,
            pl.BlockSpec(memory_space=pl.ANY), pl.BlockSpec(memory_space=pl.ANY),
        ],
        out_specs=(vmem, vmem),
        scratch_shapes=[
            pltpu.VMEM((own_tiles, width, width), f32),
            pltpu.VMEM((own_tiles, width, width), f32),
            pltpu.VMEM((own_tiles, 2 * width, 2 * width), bf16),
            pltpu.VMEM((own_tiles, 2 * width, width), bf16),
            pltpu.VMEM((fluids - 1, owners, fields, chunks, width), f32),
            pltpu.VMEM((owners - 1, fields, chunks, width), f32),
            pltpu.VMEM((owners - 1, fields, chunks, width), f32),
            pltpu.VMEM((fluids, fields, chunks, width), f32),
            pltpu.VMEM((wide, width), f32),
            pltpu.VMEM((wide, width), f32),
            pltpu.VMEM((wide, width), f32),
            pltpu.VMEM((own_tiles + reach, ROWS, width), f32),
            pltpu.VMEM((wide, width), f32),
            pltpu.VMEM((own_tiles * ROWS, width), f32),
            pltpu.VMEM((3, fields, reach, width), f32),
            pltpu.VMEM((3, fields, reach, width), f32),
            pltpu.VMEM((2, fields, reach, width), f32),
            pltpu.VMEM((2, fields, reach, width), f32),
            pltpu.VMEM((owners, ROWS, width), f32),
            dma((2,)),
            dma((fluids - 1, owners)), dma((fluids - 1, owners)),
            dma((owners - 1,)), dma((owners - 1,)),
            dma((fluids - 1,)), dma((fluids - 1,)),
            dma((3,)), dma((3,)),
            dma((2,)), dma((2,)),
            dma((owners - 1,)), dma((owners - 1,)),
        ],
        compiler_params=pltpu.CompilerParams(collective_id=0, has_side_effects=True),
        name="project",
    )(offsets, parts, offset_rows, diag, couple)


def local(
    fluid_flux, margin_blocks, block_fluid, block_solid, diag_blocks, couple_blocks, couple_offset
):
    fluids = lax.axis_size("fluid")
    owners = lax.axis_size("solid")
    parts = gather_terms(
        fluid_flux, margin_blocks, block_fluid, block_solid, fluids, owners, diag_blocks.shape[0]
    )
    return project(parts, diag_blocks, couple_blocks, couple_offset)


def solution(mesh):
    in_specs = (
        P(None, ("fluid", "solid"), None),
        P(("fluid", "solid"), None, None),
        P(("fluid", "solid")),
        P(("fluid", "solid")),
        P("solid", None, None),
        P("solid", None, None),
        P("solid"),
    )
    out_specs = (P(None, "solid", None), P(None, "solid", None))
    return jax.shard_map(local, mesh=mesh, in_specs=in_specs, out_specs=out_specs, check_vma=False)
```

time: 151 us -> 45.8 us (0.30)
  blocking collectives: 61.4 us -> 0 us
  Pallas kernels: 0 us -> 40.5 us
  matrix products: 30 us -> 0 us
  starting transfers between devices: 22.9 us -> 0 us
  waiting for transfers between devices: 17 us -> 0 us
  other arithmetic: 7.1 us -> 0 us
  local copies, waits for them, and re-layouts: 11.2 us -> 4.41 us
    psum x4 -> x0, blocking collectives: 61.4 us -> none  [the longest x3 44.6 us: two_products(): lax.psum((field_dots(residual, residual), field_dots(residual, image_fiel...]
    pallas_call x0 -> x2, Pallas kernels: none -> 40.5 us  [the longest x1 34 us: project(): pl.pallas_call(functools.partial(project_kernel, fluids, owners), out_sha...]
    dot_general x11 -> x0, matrix products: 30 us -> none  [the longest x3 10.1 us: apply_mass(): jnp.einsum('tij,ftj->fti', diag_blocks, vector, precision=highest)]
    all_to_all x2 -> x0, waiting for transfers between devices: 17 us -> none  [the longest x1 17 us: local(): lax.all_to_all(values, 'solid', split_axis=0, concat_axis=0, tiled=True)]
    all_to_all x2 -> x0, starting transfers between devices: 11.5 us -> none  [the longest x1 6.35 us: local(): lax.all_to_all(labels, 'solid', split_axis=0, concat_axis=0, tiled=True)]
    ppermute x6 -> x0, starting transfers between devices: 11.5 us -> none  [from_behind(): return lax.ppermute(block, axis, route)]
    scatter x2 -> x0, local copies, waits for them, and re-layouts: 6.36 us -> none  [the longest x1 5.27 us: local(): values = jnp.zeros((owners * capacity, fields, tile_width), jnp.float32)....]
    unnamed x29 -> x2, local copies, waits for them, and re-layouts: 0.08 us -> 2.84 us
  transfers between devices with their start and end apart: 8 -> 0, of which waited for: 1 -> 0; matrix products, arithmetic and copies ran while one was open for 20% -> 0% of each run, Pallas kernels for 0% -> 0%
where the time goes in v1:
time: 45.8 us; the launch traced here: 45.5 us
  Pallas kernels  40.5 us (88%)
  local copies, waits for them, and re-layouts  4.41 us (10%)
  between operations  0.64 us (1%)
    pallas_call x1, Pallas kernels, project(): pl.pallas_call(functools.partial(project_kernel, fluids, owners), out_sha...  34 us
    pallas_call x1, Pallas kernels, gather_terms(): pl.pallas_call(functools.partial(gather_kernel, fluids, owners, chunks, 8...  6.51 us
    unnamed x2, local copies, waits for them, and re-layouts  2.84 us
    broadcast_in_dim x3, local copies, waits for them, and re-layouts, project(): jnp.broadcast_to(offsets[:, None, None], (own_tiles, ROWS, width))  1.56 us

profile of v1, /device:TPU:0, one launch (start us, length us, event | category | flops | bytes accessed | tf_op | source)
XLA Modules:
  0.0 45.5 jit_solution(10477812633762954494)
XLA Ops:
  0.6 0.7 %broadcast_in_dim.10 = s32[32,8]{1,0:T(8,128)S(1)} broadcast(s32[32]{0:T(128)} %offsets.1), dimensions={0} | broadcast | bytes 1152 | tf_op jit(solution)/shard_map/broadcast_in_dim | solution.py:383
  1.4 0.1 broadcast_in_dim.11
  1.4 0.7 %broadcast_in_dim.12.offset_rows = s32[256,128]{1,0:T(8,128)} broadcast(s32[256]{0:T(256)S(1)} %broadcast_in_dim.11), dimensions={0} | broadcast | bytes 132096 | tf_op jit(solution)/shard_map/broadcast_in_dim | solution.py:383
  2.2 6.5 %gather_terms.1.parts = f32[4,8,3,8,128]{4,3,2,1,0:T(8,128)} custom-call(s32[160]{0:T(256)} %fluid_ids.1, s32[160]{0:T(256)} %solid_ids.1, bf16[3,64,128]{2,1,0:T(8,128)(2,1)} %flux.1, bf16[160,128,128]{2,1,0:T(8,128)(2,1)} %blocks.1), custom_call_target="tpu_custom_call" | custom-call | tf_op jit(solution)/shard_map/gather_terms/pallas_call | solution.py:60
  8.7 34.0 %project.1 = (f32[3,32,128]{2,1,0:T(8,128)}, f32[3,32,128]{2,1,0:T(8,128)}) custom-call(s32[32]{0:T(128)} %offsets.1, f32[4,8,3,8,128]{4,3,2,1,0:T(8,128)} %gather_terms.1.parts, s32[256,128]{1,0:T(8,128)} %broadcast_in_dim.12.offset_rows, f32[32,128,128]{2,1,0:T(8,128)} %diag.1, f32[32,128,128]{2,1,0:T(8,128)} %couple.1), custom_call_target="tpu_custom_call" | custom-call | tf_op jit(solution)/shard_map/project/pallas_call | solution.py:390
  42.7 1.4 %copy.11 = f32[3,32,128]{2,1,0:T(8,128)} copy(f32[3,32,128]{2,1,0:T(8,128)} %get-tuple-element.4) | data formatting | bytes 98304
  44.1 1.4 %copy.12 = f32[3,32,128]{2,1,0:T(8,128)} copy(f32[3,32,128]{2,1,0:T(8,128)} %get-tuple-element.5) | data formatting | bytes 98304

commit v2 on v1

--- a/solution.py
+++ b/solution.py
@@ -12,76 +12,28 @@
 LANES = 128
 
 
-def gather_kernel(fluids, owners, chunks, group, fluid_ids, solid_ids, flux, blocks, out, faces, total):
-    step = pl.program_id(0)
-    fields = flux.shape[0]
-    per_step = blocks.shape[0]
-    own_tiles = chunks * fluids
-
-    @pl.when(step == 0)
-    def _():
-        total[...] = jnp.zeros_like(total)
-        faces[...] = jnp.zeros_like(faces)
-        for field in range(fields):
-            faces[pl.ds(field, flux.shape[1], stride=ROWS), :] = flux[field].astype(jnp.float32)
-
-    def some(index, carry):
-        terms = []
-        for inner in range(group):
-            here = index * group + inner
-            start = pl.multiple_of(fluid_ids[step * per_step + here] * ROWS, ROWS)
-            chosen = faces[pl.ds(start, ROWS), :].astype(jnp.bfloat16)
-            terms.append(jnp.dot(chosen, blocks[here], preferred_element_type=jnp.float32))
-        for inner in range(group):
-            here = index * group + inner
-            start = pl.multiple_of(solid_ids[step * per_step + here] * ROWS, ROWS)
-            total[pl.ds(start, ROWS), :] += terms[inner]
-        return carry
-
-    lax.fori_loop(0, per_step // group, some, 0)
-
-    @pl.when(step == pl.num_programs(0) - 1)
-    def _():
-        def one_owner(owner, carry):
-            for part in range(fluids):
-                for field in range(fields):
-                    start = (owner * own_tiles + part * chunks) * ROWS + field
-                    out[part, owner, field] = total[pl.ds(start, chunks, stride=ROWS), :]
-            return carry
-
-        lax.fori_loop(0, owners, one_owner, 0)
-
-
-def gather_terms(flux, blocks, fluid_ids, solid_ids, fluids, owners, own_tiles):
-    fields, fluid_tiles, width = flux.shape
-    count = blocks.shape[0]
-    steps = 4 if count % 32 == 0 else 1
-    chunks = own_tiles // fluids
-    return pl.pallas_call(
-        functools.partial(gather_kernel, fluids, owners, chunks, 8),
-        grid=(steps,),
-        out_shape=jax.ShapeDtypeStruct((fluids, owners, fields, chunks, width), jnp.float32),
-        in_specs=[
-            pl.BlockSpec(memory_space=pltpu.SMEM),
-            pl.BlockSpec(memory_space=pltpu.SMEM),
-            pl.BlockSpec(memory_space=pltpu.VMEM),
-            pl.BlockSpec((count // steps, width, width), lambda i: (i, 0, 0)),
-        ],
-        out_specs=pl.BlockSpec(memory_space=pltpu.VMEM),
-        scratch_shapes=[
-            pltpu.VMEM((fluid_tiles * ROWS, width), jnp.float32),
-            pltpu.VMEM((owners * own_tiles * ROWS, width), jnp.float32),
-        ],
-        name="gather_terms",
-    )(fluid_ids, solid_ids, flux, blocks)
-
-
 def halves(value):
     high = value.astype(jnp.bfloat16)
     low = (value - high.astype(jnp.float32)).astype(jnp.bfloat16)
     return high, low
 
 
+def thirds(value):
+    high = value.astype(jnp.bfloat16)
+    rest = value - high.astype(jnp.float32)
+    middle = rest.astype(jnp.bfloat16)
+    low = (rest - middle.astype(jnp.float32)).astype(jnp.bfloat16)
+    return high, middle, low
+
+
+def routed(onehot, value):
+    return sum(jnp.dot(onehot, part, preferred_element_type=jnp.float32) for part in thirds(value))
+
+
+def hits(condition):
+    return jnp.where(condition, 1.0, 0.0).astype(jnp.bfloat16)
+
+
 def stacked(value):
     both = jnp.concatenate(halves(value), axis=0)
     return jnp.concatenate([both, both], axis=1)
@@ -92,24 +44,33 @@
 
 
 def project_kernel(
-    fluids, owners, offsets, parts, offset_rows, diag, couple, mapped_out, nodal_out,
-    diag_f, couple_f, first, second, got_fluid, to_owner, got_owner, mapped,
+    fluids, owners, offsets, fluid_ids, offset_row, solid_row, flux, blocks, diag, couple, outs,
+    blocks_v, faces_flat, faces, terms, parts, diag_f, couple_f, first, second, got_fluid, to_owner, got_owner, mapped,
     basis0, basis1, basis2, picks, spread, back, rim_out, rim_in, carry_out, carry_in, sums,
-    load_sem, send1, recv1, send2, recv2, send3, recv3, send_rim, recv_rim,
+    block_sem, load_sem, send1, recv1, send2, recv2, send3, recv3, send_rim, recv_rim,
     send_carry, recv_carry, send_sum, recv_sum,
 ):
     me_g = lax.axis_index("fluid")
     me_s = lax.axis_index("solid")
     fields = parts.shape[2]
     chunks = parts.shape[3]
+    mapped_out, nodal_out = outs.at[0], outs.at[1]
     own_tiles = diag.shape[0]
     reach = own_tiles // 2
     own_rows = own_tiles * ROWS
 
     load_d = pltpu.make_async_copy(diag, diag_f, load_sem.at[0])
     load_c = pltpu.make_async_copy(couple, couple_f, load_sem.at[1])
-    load_d.start()
-    load_c.start()
+    count, width = blocks.shape[0], blocks.shape[2]
+    pieces = block_sem.shape[0]
+    piece = count // pieces
+
+    def load_block(index):
+        span = pl.ds(index * piece, piece)
+        return pltpu.make_async_copy(blocks.at[span], blocks_v.at[span], block_sem.at[index])
+
+    for index in range(pieces):
+        load_block(index).start()
 
     def fluid_peer(step):
         return lax.rem(me_g + step, fluids)
@@ -126,6 +87,43 @@
         pl.semaphore_signal(
             barrier, inc=1, device_id={"fluid": me_g, "solid": solid_peer(step)}, device_id_type=MESH
         )
+
+    faces_flat[...] = jnp.zeros_like(faces_flat)
+    for field in range(fields):
+        faces_flat[pl.ds(field, flux.shape[1], stride=ROWS), :] = flux[field].astype(jnp.float32)
+    for tile in range(flux.shape[1]):
+        faces[tile] = faces_flat[tile * ROWS : (tile + 1) * ROWS, :]
+    basis0[...] = jnp.zeros_like(basis0)
+    basis1[...] = jnp.zeros_like(basis1)
+    basis2[...] = jnp.zeros_like(basis2)
+
+    for index in range(pieces):
+        load_block(index).wait()
+        if index == pieces // 2:
+            load_d.start()
+            load_c.start()
+
+        def one_term(block, carry):
+            chosen = faces[fluid_ids[block]].astype(jnp.bfloat16)
+            term = jnp.dot(chosen, blocks_v[block], preferred_element_type=jnp.float32)
+            terms[pl.ds(pl.multiple_of(block * ROWS, ROWS), ROWS), :] = term
+            return carry
+
+        lax.fori_loop(index * piece, (index + 1) * piece, one_term, 0, unroll=16)
+
+    table = jnp.concatenate(
+        [terms[pl.ds(field, count, stride=ROWS), :] for field in range(fields)], axis=1
+    )
+    span = own_tiles * max(1, min(owners, 256 // own_tiles))
+    for base in range(0, owners * own_tiles, span):
+        tiles = lax.broadcasted_iota(jnp.int32, (span, count), 0) + base
+        summed = routed(hits(tiles == solid_row[...]), table)
+        for start in range(0, span, chunks):
+            owner, part = (base + start) // own_tiles, start % own_tiles // chunks
+            for field in range(fields):
+                parts[part, owner, field] = summed[
+                    start : start + chunks, field * width : (field + 1) * width
+                ]
     pl.semaphore_wait(barrier, fluids - 1 + owners - 1)
 
     def remote(src, dst, send_sem, recv_sem, g, s):
@@ -163,10 +161,6 @@
     for step in range(1, owners + 1):
         for hop in range(1, fluids):
             copy1(hop, step).start()
-
-    basis0[...] = jnp.zeros_like(basis0)
-    basis1[...] = jnp.zeros_like(basis1)
-    basis2[...] = jnp.zeros_like(basis2)
 
     load_d.wait()
     load_c.wait()
@@ -184,7 +178,7 @@
         second[tile, LANES:, :] = turned_low
         return carry
 
-    lax.fori_loop(0, own_tiles, prepare, 0)
+    lax.fori_loop(0, own_tiles, prepare, 0, unroll=4)
 
     for step in range(1, owners + 1):
         owner = solid_peer(step)
@@ -256,18 +250,17 @@
             back[rows_of(tile), :] = product[:, LANES:]
             return carry
 
-        lax.fori_loop(0, own_tiles, own, 0, unroll=8)
-        spread[own_rows:, :] = jnp.zeros((reach * ROWS, LANES), jnp.float32)
-
-        def move(offset, carry):
-            start = pl.multiple_of(offset * ROWS, ROWS)
-            moved = jnp.where(offset_rows[...] == offset, back[...], 0.0)
-            spread[pl.ds(start, own_rows), :] += moved
-            return carry
-
-        lax.fori_loop(1, reach + 1, move, 0)
+        lax.fori_loop(0, own_tiles, own, 0, unroll=16)
+        table = jnp.concatenate(
+            [back[pl.ds(field, own_tiles, stride=ROWS), :] for field in range(fields)], axis=1
+        )
+        targets = lax.broadcasted_iota(jnp.int32, (own_tiles + reach, own_tiles), 0)
+        sources = lax.broadcasted_iota(jnp.int32, (own_tiles + reach, own_tiles), 1)
+        moved = routed(hits(sources + offset_row[...] == targets), table)
         for field in range(fields):
-            carry_out[turn, field] = spread[pl.ds(own_rows + field, reach, stride=ROWS), :]
+            lanes = slice(field * LANES, (field + 1) * LANES)
+            carry_out[turn, field] = moved[own_tiles:, lanes]
+            spread[pl.ds(field, own_tiles, stride=ROWS), :] += moved[:own_tiles, lanes]
 
         @pl.when(me_s < owners - 1)
         def _():
@@ -279,7 +272,7 @@
             image[rows_of(tile), :] = spread[rows_of(tile), :] + ahead_of(tile)
             return carry
 
-        lax.fori_loop(0, own_tiles, ahead, 0, unroll=8)
+        lax.fori_loop(0, own_tiles, ahead, 0, unroll=16)
 
         @pl.when(me_s > 0)
         def _():
@@ -300,13 +293,13 @@
         return tuple(c + a * b for c, (a, b) in zip(carry, pairs))
 
     nothing = jnp.zeros((ROWS, LANES), jnp.float32)
-    products = lax.fori_loop(0, own_tiles, dots, (nothing,) * 6, unroll=8)
+    products = lax.fori_loop(0, own_tiles, dots, (nothing,) * 6, unroll=16)
     take_rim(2, basis2)
 
     def last(tile, carry):
         return carry + 2.0 * basis2[rows_of(tile), :] * ahead_of(tile)
 
-    products = products[:5] + (lax.fori_loop(0, own_tiles, last, products[5], unroll=8),)
+    products = products[:5] + (lax.fori_loop(0, own_tiles, last, products[5], unroll=16),)
     lane = lax.broadcasted_iota(jnp.int32, (ROWS, LANES), 1)
     packed = nothing
     for place, product in enumerate(products):
@@ -376,26 +369,39 @@
             carry_copy(turn).wait_send()
 
 
-def project(parts, diag, couple, offsets):
-    fluids, owners, fields, chunks, width = parts.shape
-    own_tiles = diag.shape[0]
+def finish_kernel(both, mapped_out, nodal_out):
+    mapped_out[...] = both[0]
+    nodal_out[...] = both[1]
+
+
+def local(
+    fluid_flux, margin_blocks, block_fluid, block_solid, diag_blocks, couple_blocks, couple_offset
+):
+    fluids = lax.axis_size("fluid")
+    owners = lax.axis_size("solid")
+    fields, fluid_tiles, width = fluid_flux.shape
+    count = margin_blocks.shape[0]
+    own_tiles = diag_blocks.shape[0]
+    chunks = own_tiles // fluids
     reach = own_tiles // 2
-    offset_rows = jnp.broadcast_to(offsets[:, None, None], (own_tiles, ROWS, width))
-    offset_rows = offset_rows.reshape(own_tiles * ROWS, width)
+    pieces = count // 32 if count % 32 == 0 else 1
     f32, bf16 = jnp.float32, jnp.bfloat16
     dma = pltpu.SemaphoreType.DMA
     wide = (own_tiles + reach) * ROWS
-    out = jax.ShapeDtypeStruct((fields, own_tiles, width), f32)
     vmem = pl.BlockSpec(memory_space=pltpu.VMEM)
-    return pl.pallas_call(
+    smem = pl.BlockSpec(memory_space=pltpu.SMEM)
+    far = pl.BlockSpec(memory_space=pltpu.HBM)
+    both = pl.pallas_call(
         functools.partial(project_kernel, fluids, owners),
-        out_shape=(out, out),
-        in_specs=[
-            pl.BlockSpec(memory_space=pltpu.SMEM), vmem, vmem,
-            pl.BlockSpec(memory_space=pl.ANY), pl.BlockSpec(memory_space=pl.ANY),
-        ],
-        out_specs=(vmem, vmem),
+        out_shape=jax.ShapeDtypeStruct((2, fields, own_tiles, width), f32),
+        in_specs=[smem, smem, vmem, vmem, vmem, far, far, far],
+        out_specs=vmem,
         scratch_shapes=[
+            pltpu.VMEM((count, width, width), bf16),
+            pltpu.VMEM((fluid_tiles * ROWS, width), f32),
+            pltpu.VMEM((fluid_tiles, ROWS, width), f32),
+            pltpu.VMEM((count * ROWS, width), f32),
+            pltpu.VMEM((fluids, owners, fields, chunks, width), f32),
             pltpu.VMEM((own_tiles, width, width), f32),
             pltpu.VMEM((own_tiles, width, width), f32),
             pltpu.VMEM((own_tiles, 2 * width, 2 * width), bf16),
@@ -408,13 +414,14 @@
             pltpu.VMEM((wide, width), f32),
             pltpu.VMEM((wide, width), f32),
             pltpu.VMEM((own_tiles + reach, ROWS, width), f32),
-            pltpu.VMEM((wide, width), f32),
+            pltpu.VMEM((own_tiles * ROWS, width), f32),
             pltpu.VMEM((own_tiles * ROWS, width), f32),
             pltpu.VMEM((3, fields, reach, width), f32),
             pltpu.VMEM((3, fields, reach, width), f32),
             pltpu.VMEM((2, fields, reach, width), f32),
             pltpu.VMEM((2, fields, reach, width), f32),
             pltpu.VMEM((owners, ROWS, width), f32),
+            dma((pieces,)),
             dma((2,)),
             dma((fluids - 1, owners)), dma((fluids - 1, owners)),
             dma((owners - 1,)), dma((owners - 1,)),
@@ -423,20 +430,19 @@
             dma((2,)), dma((2,)),
             dma((owners - 1,)), dma((owners - 1,)),
         ],
-        compiler_params=pltpu.CompilerParams(collective_id=0, has_side_effects=True),
+        compiler_params=pltpu.CompilerParams(
+            collective_id=0, has_side_effects=True, vmem_limit_bytes=62400 * 1024
+        ),
         name="project",
-    )(offsets, parts, offset_rows, diag, couple)
-
-
-def local(
-    fluid_flux, margin_blocks, block_fluid, block_solid, diag_blocks, couple_blocks, couple_offset
-):
-    fluids = lax.axis_size("fluid")
-    owners = lax.axis_size("solid")
-    parts = gather_terms(
-        fluid_flux, margin_blocks, block_fluid, block_solid, fluids, owners, diag_blocks.shape[0]
+    )(
+        couple_offset, block_fluid, couple_offset[None, :], block_solid[None, :],
+        fluid_flux, margin_blocks, diag_blocks, couple_blocks,
     )
-    return project(parts, diag_blocks, couple_blocks, couple_offset)
+    out = jax.ShapeDtypeStruct((fields, own_tiles, width), f32)
+    return pl.pallas_call(
+        finish_kernel, out_shape=(out, out), in_specs=[vmem], out_specs=(vmem, vmem), name="finish",
+        compiler_params=pltpu.CompilerParams(vmem_limit_bytes=8 * 1024 * 1024),
+    )(both)
 
 
 def solution(mesh):

time: 45.8 us -> 35.6 us (0.78)
  Pallas kernels: 40.5 us -> 33.9 us
  local copies, waits for them, and re-layouts: 4.41 us -> 0.89 us
    pallas_call x2, Pallas kernels: 40.5 us -> 33.9 us  [the longest x1 33.3 us: local(): pl.pallas_call(functools.partial(project_kernel, fluids, owners), out_sha...]
    unnamed x2, local copies, waits for them, and re-layouts: 2.84 us -> 0.89 us
    broadcast_in_dim x3 -> x0, local copies, waits for them, and re-layouts: 1.56 us -> none  [project(): jnp.broadcast_to(offsets[:, None, None], (own_tiles, ROWS, width))]
where the time goes in v2:
time: 35.6 us; the launch traced here: 35.4 us
  Pallas kernels  33.9 us (95%)
  local copies, waits for them, and re-layouts  0.89 us (2%)
  between operations  0.65 us (2%)
    pallas_call x1, Pallas kernels, local(): pl.pallas_call(functools.partial(project_kernel, fluids, owners), out_sha...  33.3 us
    unnamed x2, local copies, waits for them, and re-layouts  0.89 us

profile of v2, /device:TPU:0, one launch (start us, length us, event | category | flops | bytes accessed | tf_op | source)
XLA Modules:
  0.0 35.4 jit_solution(17705642378255764010)
XLA Ops:
  0.6 33.3 %project.1.both = f32[2,3,32,128]{3,2,1,0:T(8,128)} custom-call(s32[32]{0:T(128)} %offsets.1, s32[160]{0:T(256)} %fluid_ids.1, s32[1,32]{1,0:T(1,128)} %bitcast.2, s32[1,160]{1,0:T(1,128)} %bitcast.3, bf16[3,64,128]{2,1,0:T(8,128)(2,1)} %flux.1, bf16[160,128,128]{2,1,0:T(8,128)(2,1)} %blocks.1, f32[32,128,128]{2,1,0:T(8,128)} %diag.1, f32[32,128,128]{2,1,0:T(8,128)} %couple.1), custom_call_target="tpu_custom_call" | custom-call | tf_op jit(solution)/shard_map/project/pallas_call | solution.py:394
  33.9 0.0 copy-start
  33.9 0.9 %copy-done = f32[2,3,32,128]{3,2,1,0:T(8,128)S(1)} copy-done((f32[2,3,32,128]{3,2,1,0:T(8,128)S(1)}, f32[2,3,32,128]{3,2,1,0:T(8,128)}, u32[]{:S(2)}) %copy-start) | copy-done | bytes 98328
  34.8 0.6 %finish.1 = (f32[3,32,128]{2,1,0:T(8,128)}, f32[3,32,128]{2,1,0:T(8,128)}) custom-call(f32[2,3,32,128]{3,2,1,0:T(8,128)S(1)} %copy-done), custom_call_target="tpu_custom_call" | custom-call | tf_op jit(solution)/shard_map/finish/pallas_call | solution.py:442
Async XLA Ops:
  33.9 0.9 %copy-start = (f32[2,3,32,128]{3,2,1,0:T(8,128)S(1)}, f32[2,3,32,128]{3,2,1,0:T(8,128)}, u32[]{:S(2)}) copy-start(f32[2,3,32,128]{3,2,1,0:T(8,128)} %project.1.both) | copy-start | bytes 294916

commit v3 on v2

--- a/solution.py
+++ b/solution.py
@@ -109,7 +109,7 @@
             terms[pl.ds(pl.multiple_of(block * ROWS, ROWS), ROWS), :] = term
             return carry
 
-        lax.fori_loop(index * piece, (index + 1) * piece, one_term, 0, unroll=16)
+        lax.fori_loop(index * piece, (index + 1) * piece, one_term, 0, unroll=32)
 
     table = jnp.concatenate(
         [terms[pl.ds(field, count, stride=ROWS), :] for field in range(fields)], axis=1
@@ -178,7 +178,7 @@
         second[tile, LANES:, :] = turned_low
         return carry
 
-    lax.fori_loop(0, own_tiles, prepare, 0, unroll=4)
+    lax.fori_loop(0, own_tiles, prepare, 0, unroll=8)
 
     for step in range(1, owners + 1):
         owner = solid_peer(step)
@@ -250,7 +250,7 @@
             back[rows_of(tile), :] = product[:, LANES:]
             return carry
 
-        lax.fori_loop(0, own_tiles, own, 0, unroll=16)
+        lax.fori_loop(0, own_tiles, own, 0, unroll=32)
         table = jnp.concatenate(
             [back[pl.ds(field, own_tiles, stride=ROWS), :] for field in range(fields)], axis=1
         )
@@ -272,7 +272,7 @@
             image[rows_of(tile), :] = spread[rows_of(tile), :] + ahead_of(tile)
             return carry
 
-        lax.fori_loop(0, own_tiles, ahead, 0, unroll=16)
+        lax.fori_loop(0, own_tiles, ahead, 0, unroll=32)
 
         @pl.when(me_s > 0)
         def _():
@@ -293,13 +293,13 @@
         return tuple(c + a * b for c, (a, b) in zip(carry, pairs))
 
     nothing = jnp.zeros((ROWS, LANES), jnp.float32)
-    products = lax.fori_loop(0, own_tiles, dots, (nothing,) * 6, unroll=16)
+    products = lax.fori_loop(0, own_tiles, dots, (nothing,) * 6, unroll=32)
     take_rim(2, basis2)
 
     def last(tile, carry):
         return carry + 2.0 * basis2[rows_of(tile), :] * ahead_of(tile)
 
-    products = products[:5] + (lax.fori_loop(0, own_tiles, last, products[5], unroll=16),)
+    products = products[:5] + (lax.fori_loop(0, own_tiles, last, products[5], unroll=32),)
     lane = lax.broadcasted_iota(jnp.int32, (ROWS, LANES), 1)
     packed = nothing
     for place, product in enumerate(products):

time: 35.6 us -> 35 us (0.983)
  Pallas kernels: 33.9 us -> 33.2 us
    pallas_call x1, Pallas kernels: 33.3 us -> 32.6 us  [local(): pl.pallas_call(functools.partial(project_kernel, fluids, owners), out_sha...]
where the time goes in v3:
time: 35 us; the launch traced here: 34.8 us
  Pallas kernels  33.2 us (95%)
  local copies, waits for them, and re-layouts  0.89 us (3%)
  between operations  0.65 us (2%)
    pallas_call x1, Pallas kernels, local(): pl.pallas_call(functools.partial(project_kernel, fluids, owners), out_sha...  32.6 us
    unnamed x2, local copies, waits for them, and re-layouts  0.89 us

profile of v3, /device:TPU:0, one launch (start us, length us, event | category | flops | bytes accessed | tf_op | source)
XLA Modules:
  0.0 34.8 jit_solution(12029931185784798273)
XLA Ops:
  0.6 32.6 %project.1.both = f32[2,3,32,128]{3,2,1,0:T(8,128)} custom-call(s32[32]{0:T(128)} %offsets.1, s32[160]{0:T(256)} %fluid_ids.1, s32[1,32]{1,0:T(1,128)} %bitcast.2, s32[1,160]{1,0:T(1,128)} %bitcast.3, bf16[3,64,128]{2,1,0:T(8,128)(2,1)} %flux.1, bf16[160,128,128]{2,1,0:T(8,128)(2,1)} %blocks.1, f32[32,128,128]{2,1,0:T(8,128)} %diag.1, f32[32,128,128]{2,1,0:T(8,128)} %couple.1), custom_call_target="tpu_custom_call" | custom-call | tf_op jit(solution)/shard_map/project/pallas_call | solution.py:394
  33.2 0.0 copy-start
  33.2 0.9 %copy-done = f32[2,3,32,128]{3,2,1,0:T(8,128)S(1)} copy-done((f32[2,3,32,128]{3,2,1,0:T(8,128)S(1)}, f32[2,3,32,128]{3,2,1,0:T(8,128)}, u32[]{:S(2)}) %copy-start) | copy-done | bytes 98328
  34.1 0.6 %finish.1 = (f32[3,32,128]{2,1,0:T(8,128)}, f32[3,32,128]{2,1,0:T(8,128)}) custom-call(f32[2,3,32,128]{3,2,1,0:T(8,128)S(1)} %copy-done), custom_call_target="tpu_custom_call" | custom-call | tf_op jit(solution)/shard_map/finish/pallas_call | solution.py:442
Async XLA Ops:
  33.2 0.9 %copy-start = (f32[2,3,32,128]{3,2,1,0:T(8,128)S(1)}, f32[2,3,32,128]{3,2,1,0:T(8,128)}, u32[]{:S(2)}) copy-start(f32[2,3,32,128]{3,2,1,0:T(8,128)} %project.1.both) | copy-start | bytes 294916
